TPU v7x, 32 devices: a whole 2x2x4 slice. The times are simulated.
32 devices in a mesh: elem: 8 (over z, core), lev: 4 (over y, x).
Axes of the slice: x: 2, y: 2, z: 4, core: 2. Of those that a mesh axis runs over, the one named last changes fastest.
Arguments:
- tracers: float32 [512, 16, 640], P('elem', 'lev'), may hold values from 0.1 to 120, as said below
- ref_index: int32 [512, 16], P('elem'), may hold values from 0 to 63
- requests: int32 [8, 2, 16], P('elem'), may hold values from -1 to 63, as said below
- source: int32 [512], P('elem'), may hold values from 0 to 95, as said below
- target_mean: float32 [40], replicated, may hold values from 0.5 to 5
Outputs:
- transported: float32 [512, 16, 640], P('elem', 'lev')
Inputs may be any that keep to these rules, and one draw needn't show every extreme that they name: Row 0 of requests[d] holds distinct element indices of block d - 1 (wrapping), row 1 of block d + 1; the valid entries come first and the rest are -1; every row holds 1 to 16 valid entries and some row holds exactly 16. `source`: every slot names an own element (below 64) or a valid entry of the block's requests: 64 + k for row 0, 80 + k for row 1. `tracers`: all entries are positive.
All inputs are finite; a program needn't handle non-finite values.
Results may differ from a plain program's by a relative error of at most 0.0003.
Values sent between devices are 32-bit elements; how exact they have to be, the bound alone decides.
A program may use at most 64 MiB of HBM per device.

v0:
```python
import math
import jax
import jax.numpy as jnp
from jax import lax
from jax.sharding import PartitionSpec as P

NPTS = 16
REFS = 64


def with_halo(cells, sides, width):
    for axis, dim in sides:
        count = lax.axis_size(axis)
        head = lax.slice_in_dim(cells, 0, width, axis=dim)
        tail = lax.slice_in_dim(cells, cells.shape[dim] - width, cells.shape[dim], axis=dim)
        cells = jnp.concatenate(
            [
                lax.ppermute(tail, axis, [(i, (i + 1) % count) for i in range(count)]),
                cells,
                lax.ppermute(head, axis, [((i + 1) % count, i) for i in range(count)]),
            ],
            axis=dim,
        )
    return cells


def lagrange_table():
    side = math.isqrt(REFS)
    gll_nodes = [-1.0, -math.sqrt(0.2), math.sqrt(0.2), 1.0]
    points = -1.0 + 2.0 * jnp.arange(side, dtype=jnp.float32) / (side - 1)
    columns = []
    for which in range(4):
        basis = jnp.ones((side,), jnp.float32)
        for other in range(4):
            if other != which:
                basis = basis * (points - gll_nodes[other]) / (gll_nodes[which] - gll_nodes[other])
        columns.append(basis)
    one_dim = jnp.stack(columns, axis=1)
    return (one_dim[:, None, :, None] * one_dim[None, :, None, :]).reshape(side * side, 16)


def quadrature():
    edge = jnp.array([1.0 / 6.0, 5.0 / 6.0, 5.0 / 6.0, 1.0 / 6.0], jnp.float32)
    return (edge[:, None] * edge[None, :]).reshape(16)


def interpolate(source_rows, ref_index):
    elem_count, levels, width = source_rows.shape
    onehot = (ref_index[:, :, None] == jnp.arange(REFS, dtype=jnp.int32)[None, None, :]).astype(
        jnp.float32
    )
    matrix = jnp.einsum("epr,rn->epn", onehot, lagrange_table(), precision=lax.Precision.HIGHEST)
    values = source_rows.reshape(elem_count, levels * (width // 16), 16)
    result = jnp.einsum("epn,ecn->ecp", matrix, values, precision=lax.Precision.HIGHEST)
    lowest = jnp.min(values, axis=2, keepdims=True)
    highest = jnp.max(values, axis=2, keepdims=True)
    result = jnp.minimum(jnp.maximum(result, lowest), highest)
    return result.reshape(elem_count, levels, width)


def per_device(tracers, ref_index, requests, source, target_mean):
    elem_count, levels, width = tracers.shape
    beside_all = with_halo(tracers, (("elem", 0),), elem_count)
    own_pos = jnp.arange(elem_count, 2 * elem_count, dtype=jnp.int32)
    left_pos = jnp.maximum(requests[0, 0], 0)
    right_pos = 2 * elem_count + jnp.maximum(requests[0, 1], 0)
    slot_pos = jnp.concatenate([own_pos, left_pos, right_pos])
    source_rows = beside_all[slot_pos[source]]
    clipped = interpolate(source_rows, ref_index)
    tracer_count = width // NPTS
    shaped = clipped.reshape(elem_count, levels, tracer_count, NPTS)
    local_mass = jnp.einsum("eltn,n->t", shaped, quadrature(), precision=lax.Precision.HIGHEST)
    column_mass = lax.psum(local_mass, "lev")
    global_mass = lax.psum(column_mass, "elem")
    whole_weight = 4.0 * elem_count * lax.axis_size("elem") * levels * lax.axis_size("lev")
    factor = target_mean * whole_weight / global_mass
    return (shaped * factor[None, None, :, None]).reshape(elem_count, levels, width)


def solution(mesh):
    placed = (P("elem", "lev", None), P("elem", None), P("elem", None, None), P("elem"), P())
    return jax.shard_map(
        per_device, mesh=mesh, in_specs=placed, out_specs=P("elem", "lev", None), check_vma=False
    )
```

profile of v0, /device:TPU:0, one launch (start us, length us, event | category | flops | bytes accessed | tf_op | source)
XLA Modules:
  0.0 54.3 jit_solution(1006085163537011619)
XLA Ops:
  0.0 4.5 %collective-permute-start.1 = (f32[64,4,640]{2,1,0:T(4,128)}, f32[64,4,640]{2,1,0:T(4,128)S(1)}, u32[]{:S(2)}, u32[]{:S(2)}) collective-permute-start(f32[64,4,640]{2,1,0:T(4,128)} %param.6), channel_id=1, source_target_pairs={{4,0},{8,4},{12,8},{16,12},{20,16},{24,20},{28,24},{0,28},{5,1},{9... | collective-permute-start | bytes 1966088 | tf_op jit(solution)/shard_map/ppermute | solution.py:20
  4.6 0.8 %maximum_bitcast_fusion = (s32[16]{0:T(128)S(1)}, s32[16]{0:T(128)S(1)}) fusion(s32[1,2,16]{2,1,0:T(2,128)} %param.8), kind=kLoop, calls=%fused_computation.29 | loop fusion | flops 48 | bytes 256 | tf_op jit(solution)/shard_map/max | solution.py:65
  5.4 0.1 reshape.146
  5.5 1.5 %fusion.1 = f32[64,16,16]{0,2,1:T(8,128)S(1)} fusion(f32[64,16,1]{0,1,2:T(8,128)S(1)} %reshape.146, s32[64,16]{0,1:T(8,128)} %param.7), kind=kOutput, calls=%fused_computation.8 | convolution fusion | flops 12648448 | bytes 73728 | tf_op jit(solution)/shard_map/epr,rn->epn/dot_general | solution.py:52
  7.0 1.0 %copy.23 = f32[64,16,16]{2,1,0:T(8,128)} copy(f32[64,16,16]{0,2,1:T(8,128)S(1)} %fusion.1) | data formatting | bytes 131072 | tf_op jit(solution)/shard_map/epr,rn->epn/dot_general | solution.py:52
  8.0 0.8 %broadcast_multiply_fusion.1 = f32[4,4]{1,0:T(4,128)S(1)} fusion(f32[4]{0:T(128)} %constant.76.clone), kind=kLoop, calls=%fused_computation.16 | loop fusion | flops 16 | bytes 80 | tf_op jit(solution)/shard_map/mul | solution.py:44
  8.8 0.1 reshape.147
  9.0 0.7 %compare_select_fusion.1 = s32[64]{0:T(128)S(1)} fusion(s32[64]{0:T(128)} %param.9), kind=kLoop, calls=%fused_computation.14 | loop fusion | flops 192 | bytes 512 | tf_op jit(solution)/shard_map/select_n | solution.py:68
  9.6 0.8 %gather_fusion = s32[64]{0:T(128)S(1)} fusion(s32[96]{0:T(128)S(1)} %pad_add_fusion, s32[1024]{0:T(1024)S(1)} %pad_clamp_fusion.1), kind=kCustom, calls=%fused_computation | custom fusion | bytes 768 | tf_op jit(solution)/shard_map/gather | solution.py:68
  10.4 7.6 %collective-permute-done.1 = f32[64,4,640]{2,1,0:T(4,128)S(1)} collective-permute-done((f32[64,4,640]{2,1,0:T(4,128)}, f32[64,4,640]{2,1,0:T(4,128)S(1)}, u32[]{:S(2)}, u32[]{:S(2)}) %collective-permute-start.1) | collective-permute-done | bytes 655392 | tf_op jit(solution)/shard_map/ppermute | solution.py:20
  18.0 3.0 %collective-permute-done = f32[64,4,640]{2,1,0:T(4,128)} collective-permute-done((f32[64,4,640]{2,1,0:T(4,128)}, f32[64,4,640]{2,1,0:T(4,128)}, u32[]{:S(2)}, u32[]{:S(2)}) %collective-permute-start) | collective-permute-done | bytes 655392 | tf_op jit(solution)/shard_map/ppermute | solution.py:18
  21.1 1.5 %pad_maximum_fusion = f32[192,4,640]{2,1,0:T(4,128)S(1)} fusion(f32[64,4,640]{2,1,0:T(4,128)S(1)} %collective-permute-done.1, f32[64,4,640]{2,1,0:T(4,128)S(1)} %copy-done, f32[64,4,640]{2,1,0:T(4,128)} %collective-permute-done), kind=kLoop, calls=%fused_computation.2 | loop fusion | flops 983040 | bytes 3932160 | tf_op jit(solution)/shard_map/concatenate | solution.py:16
  22.6 1.0 %gather_fusion.1 = f32[64,4,640]{2,1,0:T(4,128)S(1)} fusion(f32[192,4,640]{2,1,0:T(4,128)S(1)} %pad_maximum_fusion, s32[1024]{0:T(1024)S(1)} %pad_clamp_fusion), kind=kCustom, calls=%fused_computation.1 | custom fusion | bytes 1310976 | tf_op jit(solution)/shard_map/gather | solution.py:68
  23.5 0.4 copy.21
  24.0 0.5 fusion.7
  24.5 1.1 %copy.22 = f32[64,160,16]{1,2,0:T(8,128)S(1)} copy(f32[64,160,16]{0,2,1:T(8,128)S(1)} %bitcast.26) | data formatting | bytes 1310720 | tf_op jit(solution)/shard_map/reshape | solution.py:53
  25.8 2.1 %fusion.8 = (f32[160,16]{0,1:T(8,128)S(1)}, f32[64,160,16]{1,2,0:T(8,128)S(1)}) fusion(f32[64,160]{1,0:T(8,128)S(1)} %copy.25, f32[64,160]{1,0:T(8,128)S(1)} %copy.24, f32[64,160,16]{1,2,0:T(8,128)S(1)} %copy.22, f32[64,16,16]{2,1,0:T(8,128)} %copy.23), kind=kOutput, calls=%fused_computation.32 | convolution fusion | flops 31946240 | bytes 1468416 | tf_op jit(solution)/shard_map/epn,ecn->ecp/dot_general | solution.py:54
  28.0 0.1 reduce_sum.14
  28.1 0.1 convolution_bitcast_fusion
  28.2 9.9 %psum.14 = f32[40]{0:T(128)S(1)} all-reduce(f32[40]{0:T(128)S(1)} %convolution_bitcast_fusion), channel_id=1, replica_groups=mesh['elem'=8,'lev'=4] {'lev'}, use_global_device_ids=true, to_apply=%region_4.0 | all-reduce | flops 40 | bytes 320 | tf_op jit(solution)/shard_map/psum | solution.py:73
  38.1 13.6 %psum.15 = f32[40]{0:T(128)S(1)} all-reduce(f32[40]{0:T(128)S(1)} %psum.14), channel_id=1, replica_groups=mesh['elem'=8,'lev'=4] {'elem'}, use_global_device_ids=true, to_apply=%region_5.6 | all-reduce | flops 40 | bytes 320 | tf_op jit(solution)/shard_map/psum | solution.py:74
  51.8 1.1 %copy.26 = f32[64,160,16]{0,2,1:T(8,128)S(1)} copy(f32[64,160,16]{1,2,0:T(8,128)S(1)} %get-tuple-element.10) | data formatting | bytes 1310720 | tf_op jit(solution)/shard_map/min | solution.py:57
  52.9 0.2 bitcast_multiply_fusion
  53.1 1.2 %copy.27 = f32[64,4,640]{2,1,0:T(4,128)} copy(f32[64,4,640]{0,2,1:T(8,128)S(1)} %bitcast_multiply_fusion) | data formatting | bytes 1310720 | tf_op jit(solution)/shard_map/mul | solution.py:77
  (20 shorter events, 0.6 us)
Async XLA Ops:
  0.0 21.1 %copy-start = (f32[64,4,640]{2,1,0:T(4,128)S(1)}, f32[64,4,640]{2,1,0:T(4,128)}, u32[]{:S(2)}) copy-start(f32[64,4,640]{2,1,0:T(4,128)} %param.6) | copy-start | bytes 1966084
  0.0 18.0 %collective-permute-start.1 = (f32[64,4,640]{2,1,0:T(4,128)}, f32[64,4,640]{2,1,0:T(4,128)S(1)}, u32[]{:S(2)}, u32[]{:S(2)}) collective-permute-start(f32[64,4,640]{2,1,0:T(4,128)} %param.6), channel_id=1, source_target_pairs={{4,0},{8,4},{12,8},{16,12},{20,16},{24,20},{28,24},{0,28},{5,1},{9... | collective-permute-start | bytes 1966088 | tf_op jit(solution)/shard_map/ppermute | solution.py:20
  4.5 16.5 %collective-permute-start = (f32[64,4,640]{2,1,0:T(4,128)}, f32[64,4,640]{2,1,0:T(4,128)}, u32[]{:S(2)}, u32[]{:S(2)}) collective-permute-start(f32[64,4,640]{2,1,0:T(4,128)} %param.6), channel_id=1, source_target_pairs={{0,4},{4,8},{8,12},{12,16},{16,20},{20,24},{24,28},{28,0},{1,5},{5... | collective-permute-start | bytes 1966088 | tf_op jit(solution)/shard_map/ppermute | solution.py:18
  25.6 26.1 %copy-start.1 = (f32[40]{0:T(128)S(1)}, f32[40]{0:T(128)}, u32[]{:S(2)}) copy-start(f32[40]{0:T(128)} %param.10) | copy-start | bytes 484
where the time goes:
time: 54.6 us; the launch traced here: 54.3 us
  blocking collectives  23.5 us (43%)
  waiting for transfers between devices  10.6 us (19%)
  local copies, waits for them, and re-layouts  7.18 us (13%)
  other arithmetic  4.66 us (9%)
  starting transfers between devices  4.52 us (8%)
  matrix products  3.75 us (7%)
    psum x1, blocking collectives, per_device(): global_mass = lax.psum(column_mass, 'elem')  13.6 us
    psum x1, blocking collectives, per_device(): column_mass = lax.psum(local_mass, 'lev')  9.89 us
    ppermute x1, waiting for transfers between devices, with_halo(): lax.ppermute(head, axis, [((i + 1) % count, i) for i in range(count)])  7.59 us
    ppermute x1, starting transfers between devices, with_halo(): lax.ppermute(head, axis, [((i + 1) % count, i) for i in range(count)])  4.52 us
    ppermute x1, waiting for transfers between devices, with_halo(): lax.ppermute(tail, axis, [(i, (i + 1) % count) for i in range(count)])  3.03 us
    gather x3, local copies, waits for them, and re-layouts, per_device(): source_rows = beside_all[slot_pos[source]]  2.17 us
    dot_general x1, matrix products, interpolate(): jnp.einsum('epn,ecn->ecp', matrix, values, precision=lax.Precision.HIGHEST)  2.15 us
    concatenate x1, other arithmetic, with_halo(): jnp.concatenate([lax.ppermute(tail, axis, [(i, (i + 1) % count) for i in...  1.51 us
  transfers between devices with their start and end apart: 2, of which 2 were waited for; matrix products, arithmetic and copies ran while one was open for 11% of the time, Pallas kernels for 0%

commit v1 on v0

--- a/solution.py
+++ b/solution.py
@@ -59,6 +59,17 @@
 
 
 def per_device(tracers, ref_index, requests, source, target_mean):
+
+    def perform_zone(mine_x):
+        mesh_ax = "lev"
+        full_n = jax.lax.axis_size(mesh_ax)
+        res = lambda v1: [(jj, jj ^ v1) for jj in range(full_n)]
+        reached = mine_x
+        for b in range(full_n.bit_length() - 1):
+            z2 = jax.lax.ppermute(reached, mesh_ax, res(1 << b))
+            reached = reached + z2
+        return reached
+
     elem_count, levels, width = tracers.shape
     beside_all = with_halo(tracers, (("elem", 0),), elem_count)
     own_pos = jnp.arange(elem_count, 2 * elem_count, dtype=jnp.int32)
@@ -70,7 +81,7 @@
     tracer_count = width // NPTS
     shaped = clipped.reshape(elem_count, levels, tracer_count, NPTS)
     local_mass = jnp.einsum("eltn,n->t", shaped, quadrature(), precision=lax.Precision.HIGHEST)
-    column_mass = lax.psum(local_mass, "lev")
+    column_mass = perform_zone(local_mass)
     global_mass = lax.psum(column_mass, "elem")
     whole_weight = 4.0 * elem_count * lax.axis_size("elem") * levels * lax.axis_size("lev")
     factor = target_mean * whole_weight / global_mass

time: 54.6 us -> 50.8 us (0.930)
  blocking collectives: 23.5 us -> 13.6 us
  waiting for transfers between devices: 10.6 us -> 13.7 us
  starting transfers between devices: 4.52 us -> 7.54 us
    psum x1 -> x0, blocking collectives: 9.89 us -> none  [per_device(): column_mass = lax.psum(local_mass, 'lev')]
    ppermute x0 -> x2, waiting for transfers between devices: none -> 3.06 us  [perform_zone(): z2 = jax.lax.ppermute(reached, mesh_ax, res(1 << b))]
    ppermute x0 -> x2, starting transfers between devices: none -> 3.02 us  [perform_zone(): z2 = jax.lax.ppermute(reached, mesh_ax, res(1 << b))]
  transfers between devices with their start and end apart: 2 -> 4, of which waited for: 2 -> 4; matrix products, arithmetic and copies ran while one was open for 11% -> 14% of each run, Pallas kernels for 0% -> 0%
where the time goes in v1:
time: 50.8 us; the launch traced here: 50.5 us
  waiting for transfers between devices  13.7 us (27%)
  blocking collectives  13.6 us (27%)
  starting transfers between devices  7.54 us (15%)
  local copies, waits for them, and re-layouts  7.17 us (14%)
  other arithmetic  4.68 us (9%)
  matrix products  3.75 us (7%)
    psum x1, blocking collectives, per_device(): global_mass = lax.psum(column_mass, 'elem')  13.6 us
    ppermute x1, waiting for transfers between devices, with_halo(): lax.ppermute(head, axis, [((i + 1) % count, i) for i in range(count)])  7.59 us
    ppermute x1, starting transfers between devices, with_halo(): lax.ppermute(head, axis, [((i + 1) % count, i) for i in range(count)])  4.52 us
    ppermute x2, waiting for transfers between devices, perform_zone(): z2 = jax.lax.ppermute(reached, mesh_ax, res(1 << b))  3.06 us
    ppermute x1, waiting for transfers between devices, with_halo(): lax.ppermute(tail, axis, [(i, (i + 1) % count) for i in range(count)])  3.03 us
    ppermute x2, starting transfers between devices, perform_zone(): z2 = jax.lax.ppermute(reached, mesh_ax, res(1 << b))  3.02 us
    gather x3, local copies, waits for them, and re-layouts, per_device(): source_rows = beside_all[slot_pos[source]]  2.17 us
    dot_general x1, matrix products, interpolate(): jnp.einsum('epn,ecn->ecp', matrix, values, precision=lax.Precision.HIGHEST)  2.15 us
  transfers between devices with their start and end apart: 4, of which 4 were waited for; matrix products, arithmetic and copies ran while one was open for 14% of the time, Pallas kernels for 0%

profile of v1, /device:TPU:0, one launch (start us, length us, event | category | flops | bytes accessed | tf_op | source)
XLA Modules:
  0.0 50.5 jit_solution(17054327741406898953)
XLA Ops:
  0.0 4.5 %collective-permute-start.1 = (f32[64,4,640]{2,1,0:T(4,128)}, f32[64,4,640]{2,1,0:T(4,128)S(1)}, u32[]{:S(2)}, u32[]{:S(2)}) collective-permute-start(f32[64,4,640]{2,1,0:T(4,128)} %param.6), channel_id=1, source_target_pairs={{4,0},{8,4},{12,8},{16,12},{20,16},{24,20},{28,24},{0,28},{5,1},{9... | collective-permute-start | bytes 1966088 | tf_op jit(solution)/shard_map/ppermute | solution.py:20
  4.6 0.8 %maximum_bitcast_fusion = (s32[16]{0:T(128)S(1)}, s32[16]{0:T(128)S(1)}) fusion(s32[1,2,16]{2,1,0:T(2,128)} %param.8), kind=kLoop, calls=%fused_computation.29 | loop fusion | flops 48 | bytes 256 | tf_op jit(solution)/shard_map/max | solution.py:76
  5.5 1.5 %fusion.1 = f32[64,16,16]{0,2,1:T(8,128)S(1)} fusion(f32[64,16,1]{0,1,2:T(8,128)S(1)} %reshape.146, s32[64,16]{0,1:T(8,128)} %param.7), kind=kOutput, calls=%fused_computation.8 | convolution fusion | flops 12648448 | bytes 73728 | tf_op jit(solution)/shard_map/epr,rn->epn/dot_general | solution.py:52
  7.0 1.0 %copy.23 = f32[64,16,16]{2,1,0:T(8,128)} copy(f32[64,16,16]{0,2,1:T(8,128)S(1)} %fusion.1) | data formatting | bytes 131072 | tf_op jit(solution)/shard_map/epr,rn->epn/dot_general | solution.py:52
  8.0 0.8 %broadcast_multiply_fusion.1 = f32[4,4]{1,0:T(4,128)S(1)} fusion(f32[4]{0:T(128)} %constant.76.clone), kind=kLoop, calls=%fused_computation.16 | loop fusion | flops 16 | bytes 80 | tf_op jit(solution)/shard_map/mul | solution.py:44
  9.0 0.7 %compare_select_fusion.1 = s32[64]{0:T(128)S(1)} fusion(s32[64]{0:T(128)} %param.9), kind=kLoop, calls=%fused_computation.14 | loop fusion | flops 192 | bytes 512 | tf_op jit(solution)/shard_map/select_n | solution.py:79
  9.6 0.8 %gather_fusion = s32[64]{0:T(128)S(1)} fusion(s32[96]{0:T(128)S(1)} %pad_add_fusion, s32[1024]{0:T(1024)S(1)} %pad_clamp_fusion.1), kind=kCustom, calls=%fused_computation | custom fusion | bytes 768 | tf_op jit(solution)/shard_map/gather | solution.py:79
  10.4 7.6 %collective-permute-done.1 = f32[64,4,640]{2,1,0:T(4,128)S(1)} collective-permute-done((f32[64,4,640]{2,1,0:T(4,128)}, f32[64,4,640]{2,1,0:T(4,128)S(1)}, u32[]{:S(2)}, u32[]{:S(2)}) %collective-permute-start.1) | collective-permute-done | bytes 655392 | tf_op jit(solution)/shard_map/ppermute | solution.py:20
  18.0 3.0 %collective-permute-done = f32[64,4,640]{2,1,0:T(4,128)} collective-permute-done((f32[64,4,640]{2,1,0:T(4,128)}, f32[64,4,640]{2,1,0:T(4,128)}, u32[]{:S(2)}, u32[]{:S(2)}) %collective-permute-start) | collective-permute-done | bytes 655392 | tf_op jit(solution)/shard_map/ppermute | solution.py:18
  21.1 1.5 %pad_maximum_fusion = f32[192,4,640]{2,1,0:T(4,128)S(1)} fusion(f32[64,4,640]{2,1,0:T(4,128)S(1)} %collective-permute-done.1, f32[64,4,640]{2,1,0:T(4,128)S(1)} %copy-done, f32[64,4,640]{2,1,0:T(4,128)} %collective-permute-done), kind=kLoop, calls=%fused_computation.2 | loop fusion | flops 983040 | bytes 3932160 | tf_op jit(solution)/shard_map/concatenate | solution.py:16
  22.6 1.0 %gather_fusion.1 = f32[64,4,640]{2,1,0:T(4,128)S(1)} fusion(f32[192,4,640]{2,1,0:T(4,128)S(1)} %pad_maximum_fusion, s32[1024]{0:T(1024)S(1)} %pad_clamp_fusion), kind=kCustom, calls=%fused_computation.1 | custom fusion | bytes 1310976 | tf_op jit(solution)/shard_map/gather | solution.py:79
  23.5 0.4 copy.21
  24.0 0.5 %fusion.7 = (f32[64,160]{0,1:T(8,128)S(1)}, f32[64,160]{0,1:T(8,128)S(1)}) fusion(f32[64,160,16]{0,2,1:T(8,128)S(1)} %bitcast.25), kind=kLoop, calls=%fused_computation.31 | loop fusion | flops 307200 | bytes 737280 | tf_op jit(solution)/shard_map/reduce_min | solution.py:55
  24.5 1.1 %copy.22 = f32[64,160,16]{1,2,0:T(8,128)S(1)} copy(f32[64,160,16]{0,2,1:T(8,128)S(1)} %bitcast.26) | data formatting | bytes 1310720 | tf_op jit(solution)/shard_map/reshape | solution.py:53
  25.8 2.1 %fusion.8 = (f32[160,16]{0,1:T(8,128)S(1)}, f32[64,160,16]{1,2,0:T(8,128)S(1)}) fusion(f32[64,160]{1,0:T(8,128)S(1)} %copy.25, f32[64,160]{1,0:T(8,128)S(1)} %copy.24, f32[64,160,16]{1,2,0:T(8,128)S(1)} %copy.22, f32[64,16,16]{2,1,0:T(8,128)} %copy.23), kind=kOutput, calls=%fused_computation.32 | convolution fusion | flops 31946240 | bytes 1468416 | tf_op jit(solution)/shard_map/epn,ecn->ecp/dot_general | solution.py:54
  28.1 0.1 convolution_bitcast_fusion
  28.2 1.5 %collective-permute-start.2 = (f32[40]{0:T(128)S(1)}, f32[40]{0:T(128)S(1)}, u32[]{:S(2)}, u32[]{:S(2)}) collective-permute-start(f32[40]{0:T(128)S(1)} %convolution_bitcast_fusion), channel_id=1, source_target_pairs={{0,1},{1,0},{2,3},{3,2},{4,5},{5,4},{6,7},{7,6},{8,9},{9,8},{10,11... | collective-permute-start | bytes 488 | tf_op jit(solution)/shard_map/ppermute | solution.py:69
  29.7 2.1 %collective-permute-done.2 = f32[40]{0:T(128)S(1)} collective-permute-done((f32[40]{0:T(128)S(1)}, f32[40]{0:T(128)S(1)}, u32[]{:S(2)}, u32[]{:S(2)}) %collective-permute-start.2) | collective-permute-done | bytes 192 | tf_op jit(solution)/shard_map/ppermute | solution.py:69
  31.8 1.5 %collective-permute-start.3 = (f32[40]{0:T(128)S(1)}, f32[40]{0:T(128)S(1)}, u32[]{:S(2)}, u32[]{:S(2)}) collective-permute-start(f32[40]{0:T(128)S(1)} %add.116), channel_id=1, source_target_pairs={{0,2},{1,3},{2,0},{3,1},{4,6},{5,7},{6,4},{7,5},{8,10},{9,11},{10,... | collective-permute-start | bytes 488 | tf_op jit(solution)/shard_map/ppermute | solution.py:69
  33.3 1.1 %copy.26 = f32[64,160,16]{0,2,1:T(8,128)S(1)} copy(f32[64,160,16]{1,2,0:T(8,128)S(1)} %get-tuple-element.10) | data formatting | bytes 1310720 | tf_op jit(solution)/shard_map/min | solution.py:57
  34.4 1.0 %collective-permute-done.3 = f32[40]{0:T(128)S(1)} collective-permute-done((f32[40]{0:T(128)S(1)}, f32[40]{0:T(128)S(1)}, u32[]{:S(2)}, u32[]{:S(2)}) %collective-permute-start.3) | collective-permute-done | bytes 192 | tf_op jit(solution)/shard_map/ppermute | solution.py:69
  35.4 13.6 %psum.7 = f32[40]{0:T(128)S(1)} all-reduce(f32[40]{0:T(128)S(1)} %add.117), channel_id=1, replica_groups=mesh['elem'=8,'lev'=4] {'elem'}, use_global_device_ids=true, to_apply=%region_4.5 | all-reduce | flops 40 | bytes 320 | tf_op jit(solution)/shard_map/psum | solution.py:85
  49.1 0.2 bitcast_multiply_fusion
  49.3 1.2 %copy.27 = f32[64,4,640]{2,1,0:T(4,128)} copy(f32[64,4,640]{0,2,1:T(8,128)S(1)} %bitcast_multiply_fusion) | data formatting | bytes 1310720 | tf_op jit(solution)/shard_map/mul | solution.py:88
  (25 shorter events, 0.8 us)
Async XLA Ops:
  0.0 21.1 %copy-start = (f32[64,4,640]{2,1,0:T(4,128)S(1)}, f32[64,4,640]{2,1,0:T(4,128)}, u32[]{:S(2)}) copy-start(f32[64,4,640]{2,1,0:T(4,128)} %param.6) | copy-start | bytes 1966084
  0.0 18.0 %collective-permute-start.1 = (f32[64,4,640]{2,1,0:T(4,128)}, f32[64,4,640]{2,1,0:T(4,128)S(1)}, u32[]{:S(2)}, u32[]{:S(2)}) collective-permute-start(f32[64,4,640]{2,1,0:T(4,128)} %param.6), channel_id=1, source_target_pairs={{4,0},{8,4},{12,8},{16,12},{20,16},{24,20},{28,24},{0,28},{5,1},{9... | collective-permute-start | bytes 1966088 | tf_op jit(solution)/shard_map/ppermute | solution.py:20
  4.5 16.5 %collective-permute-start = (f32[64,4,640]{2,1,0:T(4,128)}, f32[64,4,640]{2,1,0:T(4,128)}, u32[]{:S(2)}, u32[]{:S(2)}) collective-permute-start(f32[64,4,640]{2,1,0:T(4,128)} %param.6), channel_id=1, source_target_pairs={{0,4},{4,8},{8,12},{12,16},{16,20},{20,24},{24,28},{28,0},{1,5},{5... | collective-permute-start | bytes 1966088 | tf_op jit(solution)/shard_map/ppermute | solution.py:18
  25.8 23.1 %copy-start.1 = (f32[40]{0:T(128)S(1)}, f32[40]{0:T(128)}, u32[]{:S(2)}) copy-start(f32[40]{0:T(128)} %param.10) | copy-start | bytes 484
  28.2 3.6 %collective-permute-start.2 = (f32[40]{0:T(128)S(1)}, f32[40]{0:T(128)S(1)}, u32[]{:S(2)}, u32[]{:S(2)}) collective-permute-start(f32[40]{0:T(128)S(1)} %convolution_bitcast_fusion), channel_id=1, source_target_pairs={{0,1},{1,0},{2,3},{3,2},{4,5},{5,4},{6,7},{7,6},{8,9},{9,8},{10,11... | collective-permute-start | bytes 488 | tf_op jit(solution)/shard_map/ppermute | solution.py:69
  31.8 3.6 %collective-permute-start.3 = (f32[40]{0:T(128)S(1)}, f32[40]{0:T(128)S(1)}, u32[]{:S(2)}, u32[]{:S(2)}) collective-permute-start(f32[40]{0:T(128)S(1)} %add.116), channel_id=1, source_target_pairs={{0,2},{1,3},{2,0},{3,1},{4,6},{5,7},{6,4},{7,5},{8,10},{9,11},{10,... | collective-permute-start | bytes 488 | tf_op jit(solution)/shard_map/ppermute | solution.py:69
